TPU v7x, 256 devices: a whole 4x4x8 slice. The times are simulated.
256 devices in a mesh: seq: 64 (over z, y, core), head: 4 (over x).
Axes of the slice: x: 4, y: 4, z: 8, core: 2. Of those that a mesh axis runs over, the one named last changes fastest.
Arguments:
- query_rows: bfloat16 [131072, 4096], P(('seq', 'head')), may hold values from -200 to 200
- key_rows: bfloat16 [131072, 512], P(('seq', 'head')), may hold values from -18 to 18
- value_rows: bfloat16 [131072, 512], P(('seq', 'head')), may hold values from -6 to 6
- random_table: int32 [1024, 4, 3], replicated, may hold values from 0 to 1023, as said below
- global_blocks: int32 [2], replicated, may hold values from 0 to 1023
Outputs:
- attended: bfloat16 [131072, 4096], P(('seq', 'head'))
Inputs may be any that keep to these rules, and one draw needn't show every extreme that they name: `random_table`: for each of the 4 head groups and each aligned run of 16 query blocks (those of one index of seq), with the owner of block j being j // 16: at most 2 of the run's 3 * 16 entries name blocks of one owner, and they name at most 1 distinct blocks of one owner; both bounds are reached.
All inputs are finite; a program needn't handle non-finite values.
Results may differ from a plain program's by a relative error of at most 0.0029.
Values may be sent and summed in bfloat16 or wider, within the bound.
A program may use at most 128 MiB of HBM per device.

v0:
```python
import math
import jax
import jax.numpy as jnp
from jax import lax
from jax.sharding import PartitionSpec as P

BLOCK = 128
HEAD_DIM = 128
GLOBALS = 2
RANDOM = 3


def padded_2(cells, sides, width):
    for axis, dim in sides:
        count = lax.axis_size(axis)
        ends = count - 1
        head = lax.slice_in_dim(cells, 0, width, axis=dim)
        tail = lax.slice_in_dim(cells, cells.shape[dim] - width, cells.shape[dim], axis=dim)
        cells = jnp.concatenate(
            [
                lax.ppermute(tail, axis, [(i, (i + 1) % count) for i in range(ends)]),
                cells,
                lax.ppermute(head, axis, [((i + 1) % count, i) for i in range(ends)]),
            ],
            axis=dim,
        )
    return cells


def picked(shard, axis, root):
    return lax.dynamic_index_in_dim(lax.all_gather(shard, axis), root, 0, keepdims=False)


def attend_group(query_group, context, usable, score_scale):
    key_part = context[..., :HEAD_DIM]
    values = context[..., HEAD_DIM:]
    scores = (
        jnp.einsum("ptgd,psd->pgts", query_group, key_part, preferred_element_type=jnp.float32)
        * score_scale
    )
    scores = jnp.where(usable[:, None, None, :], scores, -1e30)
    row_max = jnp.max(scores, axis=-1, keepdims=True)
    weights = jnp.exp(scores - row_max)
    row_total = jnp.sum(weights, axis=-1)
    rounded = weights.astype(jnp.bfloat16)
    mixed = jnp.einsum("pgts,psd->ptgd", rounded, values, preferred_element_type=jnp.float32)
    mixed = mixed / jnp.transpose(row_total, (0, 2, 1))[..., None]
    return mixed.astype(jnp.bfloat16)


def on_device(query_rows, key_rows, value_rows, random_table, global_blocks):
    queries, key_part, values = (
        lax.all_to_all(query_rows, "head", split_axis=1, concat_axis=0, tiled=True),
        lax.all_to_all(key_rows, "head", split_axis=1, concat_axis=0, tiled=True),
        lax.all_to_all(value_rows, "head", split_axis=1, concat_axis=0, tiled=True),
    )
    local_rows = queries.shape[0]
    block_count = local_rows // BLOCK
    grouping = queries.shape[1] // HEAD_DIM
    seq_count = lax.axis_size("seq")
    seq_index = lax.axis_index("seq")
    head_index = lax.axis_index("head")
    paired = jnp.concatenate([key_part, values], axis=1)
    local_blocks = paired.reshape(block_count, BLOCK, 2 * HEAD_DIM)
    padded = padded_2(paired, (("seq", 0),), BLOCK)
    global_parts = []
    for global_index in range(GLOBALS):
        named_block = global_blocks[global_index]
        piece = lax.dynamic_index_in_dim(local_blocks, named_block % block_count, 0, keepdims=False)
        global_parts.append(picked(piece, "seq", named_block // block_count))
    shared = jnp.stack(global_parts)
    table_head = lax.dynamic_index_in_dim(random_table, head_index, 1, keepdims=False)
    all_refs = table_head.reshape(seq_count, block_count * RANDOM)
    my_refs = lax.dynamic_index_in_dim(all_refs, seq_index, 0, keepdims=False)
    owner_all = all_refs // block_count
    local_all = all_refs % block_count
    my_owner = my_refs // block_count
    my_local = my_refs % block_count
    entry_bound = 2 * max(1, (RANDOM * block_count + 2 * seq_count - 1) // (2 * seq_count))
    capacity = entry_bound // 2
    block_range = jnp.arange(block_count, dtype=jnp.int32)
    hits = (owner_all[:, :, None] == seq_index) & (local_all[:, :, None] == block_range)
    requested = jnp.any(hits, axis=1)
    distinct_rank = jnp.cumsum(requested.astype(jnp.int32), axis=1) - 1
    selected = requested[:, :, None] & (
        distinct_rank[:, :, None] == jnp.arange(capacity, dtype=jnp.int32)
    )
    sources = jnp.sum(jnp.where(selected, block_range[None, :, None], 0), axis=1)
    filled = jnp.any(selected, axis=1)
    outgoing = jnp.take(local_blocks, sources, axis=0)
    outgoing = jnp.where(filled[:, :, None, None], outgoing, jnp.zeros_like(outgoing))
    received = lax.all_to_all(outgoing, "seq", split_axis=0, concat_axis=0, tiled=True)
    my_requested = jnp.any(
        my_refs[:, None] == jnp.arange(seq_count * block_count, dtype=jnp.int32)[None, :], axis=0
    )
    owner_lines = my_requested.reshape(seq_count, block_count)[my_owner]
    my_slot = jnp.sum(
        (owner_lines & (block_range[None, :] < my_local[:, None])).astype(jnp.int32), axis=1
    )
    fetched = received[my_owner, my_slot].reshape(block_count, RANDOM * BLOCK, 2 * HEAD_DIM)
    previous = padded[:local_rows].reshape(block_count, BLOCK, 2 * HEAD_DIM)
    upcoming = padded[2 * BLOCK :].reshape(block_count, BLOCK, 2 * HEAD_DIM)
    shared_all = jnp.broadcast_to(
        shared.reshape(1, GLOBALS * BLOCK, 2 * HEAD_DIM),
        (block_count, GLOBALS * BLOCK, 2 * HEAD_DIM),
    )
    context = jnp.concatenate([previous, local_blocks, upcoming, shared_all, fetched], axis=1)
    global_ids = seq_index * block_count + jnp.arange(block_count, dtype=jnp.int32)
    block_flags = jnp.concatenate(
        [
            (global_ids > 0)[:, None],
            (global_ids >= 0)[:, None],
            (global_ids < seq_count * block_count - 1)[:, None],
            jnp.ones((block_count, GLOBALS + RANDOM), dtype=bool),
        ],
        axis=1,
    )
    usable = jnp.repeat(block_flags, BLOCK, axis=1)
    per_step = max((size_try for size_try in (1, 2, 3, 4) if block_count % size_try == 0))
    step_count = block_count // per_step
    score_scale = 1.0 / math.sqrt(HEAD_DIM)
    query_steps = queries.reshape(step_count, per_step, BLOCK, grouping, HEAD_DIM)
    context_steps = context.reshape(step_count, per_step, context.shape[1], 2 * HEAD_DIM)
    usable_steps = usable.reshape(step_count, per_step, usable.shape[1])

    def one_step(inputs):
        return attend_group(inputs[0], inputs[1], inputs[2], score_scale)

    mixed = lax.map(one_step, (query_steps, context_steps, usable_steps))
    output_rows = mixed.reshape(local_rows, grouping * HEAD_DIM)
    return lax.all_to_all(output_rows, "head", split_axis=0, concat_axis=1, tiled=True)


def solution(mesh):
    placed = (
        P(("seq", "head"), None),
        P(("seq", "head"), None),
        P(("seq", "head"), None),
        P(),
        P(),
    )
    return jax.shard_map(
        on_device, mesh=mesh, in_specs=placed, out_specs=P(("seq", "head"), None), check_vma=False
    )
```

profile of v0, /device:TPU:1, one launch (start us, length us, event | category | flops | bytes accessed | tf_op | source)
XLA Modules:
  0.0 373.1 jit_solution(15213330352972939691)
XLA Ops:
  8.5 4.8 %all-to-all-start = ((bf16[512,4,128]{2,0,1:T(8,128)(2,1)}), bf16[512,4,128]{2,0,1:T(8,128)(2,1)S(1)}, u32[]{:S(2)}, u32[]{:S(2)}) async-start(bf16[512,4,128]{2,0,1:T(8,128)(2,1)} %copy_bitcast_fusion.4), calls=%async_computation | async-start | bytes 1048576 | tf_op jit(solution)/shard_map/all_to_all | solution.py:54
  15.2 5.5 %all-to-all-done = bf16[512,4,128]{2,0,1:T(8,128)(2,1)S(1)} async-done(((bf16[512,4,128]{2,0,1:T(8,128)(2,1)}), bf16[512,4,128]{2,0,1:T(8,128)(2,1)S(1)}, u32[]{:S(2)}, u32[]{:S(2)}) %all-to-all-start) | async-done | bytes 524320 | tf_op jit(solution)/shard_map/all_to_all | solution.py:54
  20.8 3.5 all-to-all-start.1
  31.8 4.7 %copy.90 = bf16[64,4,8,1024]{3,2,0,1:T(8,128)(2,1)} copy(bf16[64,4,8,1024]{3,2,1,0:T(8,128)(2,1)} %bitcast.165) | data formatting | bytes 8388608 | tf_op jit(solution)/shard_map/all_to_all | solution.py:53
  36.6 4.9 %all-to-all-start.3 = ((bf16[512,4,1024]{2,0,1:T(8,128)(2,1)}), bf16[512,4,1024]{2,0,1:T(8,128)(2,1)}, u32[]{:S(2)}, u32[]{:S(2)}) async-start(bf16[512,4,1024]{2,0,1:T(8,128)(2,1)} %bitcast.159), calls=%async_computation.3 | async-start | bytes 8388608 | tf_op jit(solution)/shard_map/all_to_all | solution.py:53
  43.9 2.8 gather_fusion
  46.7 4.0 %fusion.16 = bf16[64,1,128,256]{3,2,1,0:T(8,128)(2,1)} fusion(bf16[64,128,256]{2,1,0:T(8,128)(2,1)} %gather_fusion, pred[64]{0:T(512)(128)(4,1)S(1)} %compare_and_fusion, pred[64]{0:T(512)(128)(4,1)S(1)} %get-tuple-element.70), kind=kLoop, calls=%fused_computation.27 | loop fusion | flops 4194304 | bytes 8388736 | tf_op jit(solution)/shard_map/jit(_where)/select_n | solution.py:91
  50.7 35.6 %all-to-all-done.3 = bf16[512,4,1024]{2,0,1:T(8,128)(2,1)} async-done(((bf16[512,4,1024]{2,0,1:T(8,128)(2,1)}), bf16[512,4,1024]{2,0,1:T(8,128)(2,1)}, u32[]{:S(2)}, u32[]{:S(2)}) %all-to-all-start.3) | async-done | bytes 4194336 | tf_op jit(solution)/shard_map/all_to_all | solution.py:53
  86.3 17.9 %all-to-all-start.2 = ((bf16[64,1,128,256]{3,2,1,0:T(8,128)(2,1)}), bf16[64,1,128,256]{3,2,1,0:T(8,128)(2,1)}, u32[]{:S(2)}, u32[]{:S(2)}) async-start(bf16[64,1,128,256]{3,2,1,0:T(8,128)(2,1)} %fusion.16), calls=%async_computation.2 | async-start | bytes 8388608 | tf_op jit(solution)/shard_map/all_to_all | solution.py:92
  105.5 3.5 collective-permute-start
  114.5 2.6 collective-permute-done.1
  120.6 5.2 %copy.82 = bf16[256,8,8,128]{3,2,1,0:T(8,128)(2,1)} copy(bf16[256,8,8,128]{3,1,2,0:T(8,128)(2,1)} %bitcast.53) | data formatting | bytes 8388608
  126.6 88.3 %all-gather.3.cloned.1.call-done = bf16[64,128,256]{2,1,0:T(8,128)(2,1)} async-done(((bf16[1,128,256]{2,1,0:T(8,128)(2,1)}), bf16[64,128,256]{2,1,0:T(8,128)(2,1)}) %all-gather.3.cloned.1.call-update) | async-done | bytes 4194320 | tf_op jit(solution)/shard_map/all_gather | solution.py:31
  217.4 4.6 %gather_fusion.2 = bf16[48,128,256]{2,1,0:T(8,128)(2,1)} fusion(bf16[64,1,128,256]{3,2,1,0:T(8,128)(2,1)} %all-to-all-done.2, s32[48]{0:T(128)S(1)} %fusion.35), kind=kCustom, calls=%fused_computation.2 | custom fusion | bytes 6291840 | tf_op jit(solution)/shard_map/gather | solution.py:100
  222.0 3.8 %constant_dynamic-update-slice_fusion.1 = bf16[4,4,1024,256]{3,2,1,0:T(8,128)(2,1)} fusion(bf16[4,4,1024,256]{3,2,1,0:T(8,128)(2,1)} %broadcast_dynamic-update-slice_fusion, bf16[4,4,384,256]{3,2,1,0:T(8,128)(2,1)} %bitcast.162), kind=kLoop, calls=%fused_computation.66 | loop fusion | bytes 6291456 | tf_op jit(solution)/shard_map/concatenate | solution.py:107
  225.8 66.2 %while.10 = (s32[]{:T(128)}, bf16[4,4,128,8,128]{4,3,2,1,0:T(8,128)(2,1)}, bf16[4,4,1024,256]{3,2,1,0:T(8,128)(2,1)}, pred[4,4,1024]{2,1,0:T(4,128)(4,1)S(1)}, bf16[4,4,128,8,128]{4,3,2,1,0:T(8,128)(2,1)}, /*index=5*/s32[]{:T(128)}) while((s32[]{:T(128)}, bf16[4,4,128,8,128]{4,3,2,1,0:T(8,128)(2,1)}, bf16[4,4,1024,256]{3,2,1,0:T(8,128)(2,1)}, ...), condition=%wide.region_9.10_spmd, body=%wide.region_6.9_spmd.sunk | while | flops 2194661376 | bytes 65114704 | solution.py:129
  228.9 3.0 bitcast_reduce_fusion.2
  231.9 3.7 %fusion.48 = f32[4,8,128]{2,1,0:T(8,128)S(1)} fusion(f32[4,1024,128,8]{2,1,3,0:T(8,128)S(1)} %get-tuple-element.117, f32[4,8,128]{2,1,0:T(8,128)S(1)} %get-tuple-element.118, pred[4,1024]{1,0:T(4,128)(4,1)S(1)} %dynamic-slice_bitcast_fusion.4), kind=kLoop, calls=%fused_computation.7.clone.1 | loop fusion | flops 16773120 | bytes 16814080 | tf_op jit(solution)/shard_map/while/body/eval_jaxpr/reduce_sum | solution.py:44
  235.7 4.9 %fusion.49 = bf16[1,4,128,8,128]{2,4,3,1,0:T(8,128)(2,1)S(1)} fusion(f32[4,1024,128,8]{2,1,3,0:T(8,128)S(1)} %get-tuple-element.117, f32[4,8,128]{2,1,0:T(8,128)S(1)} %get-tuple-element.118, pred[4,1024]{1,0:T(4,128)(4,1)S(1)} %dynamic-slice_bitcast_fusion.4, bf16[4,1024,256]{2,1,0:T(8,128)(2,1)S(1)} %dynamic-slice_bitcast_fusion.5, ...), kind=kOutput, calls=%fused_computation.14.clone.1 | convolution fusion | flops 1091567616 | bytes 18911232 | tf_op jit(solution)/shard_map/while/body/eval_jaxpr/pgts,psd->ptgd/dot_general | solution.py:46
  245.4 3.0 bitcast_reduce_fusion.2
  248.5 3.7 %fusion.48 = f32[4,8,128]{2,1,0:T(8,128)S(1)} fusion(f32[4,1024,128,8]{2,1,3,0:T(8,128)S(1)} %get-tuple-element.117, f32[4,8,128]{2,1,0:T(8,128)S(1)} %get-tuple-element.118, pred[4,1024]{1,0:T(4,128)(4,1)S(1)} %dynamic-slice_bitcast_fusion.4), kind=kLoop, calls=%fused_computation.7.clone.1 | loop fusion | flops 16773120 | bytes 16814080 | tf_op jit(solution)/shard_map/while/body/eval_jaxpr/reduce_sum | solution.py:44
  252.2 4.9 %fusion.49 = bf16[1,4,128,8,128]{2,4,3,1,0:T(8,128)(2,1)S(1)} fusion(f32[4,1024,128,8]{2,1,3,0:T(8,128)S(1)} %get-tuple-element.117, f32[4,8,128]{2,1,0:T(8,128)S(1)} %get-tuple-element.118, pred[4,1024]{1,0:T(4,128)(4,1)S(1)} %dynamic-slice_bitcast_fusion.4, bf16[4,1024,256]{2,1,0:T(8,128)(2,1)S(1)} %dynamic-slice_bitcast_fusion.5, ...), kind=kOutput, calls=%fused_computation.14.clone.1 | convolution fusion | flops 1091567616 | bytes 18911232 | tf_op jit(solution)/shard_map/while/body/eval_jaxpr/pgts,psd->ptgd/dot_general | solution.py:46
  262.0 3.0 bitcast_reduce_fusion.2
  265.0 3.7 %fusion.48 = f32[4,8,128]{2,1,0:T(8,128)S(1)} fusion(f32[4,1024,128,8]{2,1,3,0:T(8,128)S(1)} %get-tuple-element.117, f32[4,8,128]{2,1,0:T(8,128)S(1)} %get-tuple-element.118, pred[4,1024]{1,0:T(4,128)(4,1)S(1)} %dynamic-slice_bitcast_fusion.4), kind=kLoop, calls=%fused_computation.7.clone.1 | loop fusion | flops 16773120 | bytes 16814080 | tf_op jit(solution)/shard_map/while/body/eval_jaxpr/reduce_sum | solution.py:44
  268.8 5.0 %fusion.49 = bf16[1,4,128,8,128]{2,4,3,1,0:T(8,128)(2,1)S(1)} fusion(f32[4,1024,128,8]{2,1,3,0:T(8,128)S(1)} %get-tuple-element.117, f32[4,8,128]{2,1,0:T(8,128)S(1)} %get-tuple-element.118, pred[4,1024]{1,0:T(4,128)(4,1)S(1)} %dynamic-slice_bitcast_fusion.4, bf16[4,1024,256]{2,1,0:T(8,128)(2,1)S(1)} %dynamic-slice_bitcast_fusion.5, ...), kind=kOutput, calls=%fused_computation.14.clone.1 | convolution fusion | flops 1091567616 | bytes 18911232 | tf_op jit(solution)/shard_map/while/body/eval_jaxpr/pgts,psd->ptgd/dot_general | solution.py:46
  278.5 3.0 bitcast_reduce_fusion.2
  281.6 3.7 %fusion.48 = f32[4,8,128]{2,1,0:T(8,128)S(1)} fusion(f32[4,1024,128,8]{2,1,3,0:T(8,128)S(1)} %get-tuple-element.117, f32[4,8,128]{2,1,0:T(8,128)S(1)} %get-tuple-element.118, pred[4,1024]{1,0:T(4,128)(4,1)S(1)} %dynamic-slice_bitcast_fusion.4), kind=kLoop, calls=%fused_computation.7.clone.1 | loop fusion | flops 16773120 | bytes 16814080 | tf_op jit(solution)/shard_map/while/body/eval_jaxpr/reduce_sum | solution.py:44
  285.3 5.0 %fusion.49 = bf16[1,4,128,8,128]{2,4,3,1,0:T(8,128)(2,1)S(1)} fusion(f32[4,1024,128,8]{2,1,3,0:T(8,128)S(1)} %get-tuple-element.117, f32[4,8,128]{2,1,0:T(8,128)S(1)} %get-tuple-element.118, pred[4,1024]{1,0:T(4,128)(4,1)S(1)} %dynamic-slice_bitcast_fusion.4, bf16[4,1024,256]{2,1,0:T(8,128)(2,1)S(1)} %dynamic-slice_bitcast_fusion.5, ...), kind=kOutput, calls=%fused_computation.14.clone.1 | convolution fusion | flops 1091567616 | bytes 18911232 | tf_op jit(solution)/shard_map/while/body/eval_jaxpr/pgts,psd->ptgd/dot_general | solution.py:46
  292.1 7.3 %all_to_all.69 = bf16[4,512,1024]{2,1,0:T(8,128)(2,1)} reshape(bf16[4,4,128,8,128]{4,3,2,1,0:T(8,128)(2,1)} %get-tuple-element.32) | data formatting | bytes 8388608 | tf_op jit(solution)/shard_map/all_to_all | solution.py:131
  299.4 54.3 %all_to_all.78 = bf16[4,512,1024]{2,1,0:T(8,128)(2,1)} all-to-all(bf16[4,512,1024]{2,1,0:T(8,128)(2,1)} %all_to_all.69), channel_id=1, replica_groups=mesh['seq'=64,'head'=4] {'head'}, dimensions={0} | all-to-all | bytes 8388608 | tf_op jit(solution)/shard_map/all_to_all | solution.py:131
  353.7 6.3 %copy.69 = bf16[512,4,1024]{0,2,1:T(8,128)(2,1)} copy(bf16[512,4,1024]{2,0,1:T(8,128)(2,1)} %bitcast.160) | data formatting | bytes 8388608 | tf_op jit(solution)/shard_map/all_to_all | solution.py:131
  359.9 6.4 %copy.70 = bf16[512,4096]{1,0:T(8,128)(2,1)} copy(bf16[512,4096]{0,1:T(8,128)(2,1)} %bitcast.161) | data formatting | bytes 8388608 | tf_op jit(solution)/shard_map/all_to_all | solution.py:131
  (81 shorter events, 41.0 us)
Async XLA Ops:
  6.5 1.0 copy-start
  6.5 17.8 %copy-start.2 = (s32[2]{0:T(128)S(1)}, s32[2]{0:T(128)}, u32[]{:S(2)}) copy-start(s32[2]{0:T(128)} %param.11) | copy-start | bytes 28
  8.5 12.3 %all-to-all-start = ((bf16[512,4,128]{2,0,1:T(8,128)(2,1)}), bf16[512,4,128]{2,0,1:T(8,128)(2,1)S(1)}, u32[]{:S(2)}, u32[]{:S(2)}) async-start(bf16[512,4,128]{2,0,1:T(8,128)(2,1)} %copy_bitcast_fusion.4), calls=%async_computation | async-start | bytes 1048576 | tf_op jit(solution)/shard_map/all_to_all | solution.py:54
  20.8 10.4 %all-to-all-start.1 = ((bf16[512,4,128]{2,0,1:T(8,128)(2,1)}), bf16[512,4,128]{2,0,1:T(8,128)(2,1)S(1)}, u32[]{:S(2)}, u32[]{:S(2)}) async-start(bf16[512,4,128]{2,0,1:T(8,128)(2,1)} %copy_bitcast_fusion.3), calls=%async_computation.1 | async-start | bytes 1048576 | tf_op jit(solution)/shard_map/all_to_all | solution.py:55
  24.2 101.6 %all-gather.5.cloned.1.call-start = ((), (), s32[]{:S(2)}) async-start(), calls=%async_computation.6 | async-start | bytes 4259840 | tf_op jit(solution)/shard_map/all_gather | solution.py:31
  36.6 49.8 %all-to-all-start.3 = ((bf16[512,4,1024]{2,0,1:T(8,128)(2,1)}), bf16[512,4,1024]{2,0,1:T(8,128)(2,1)}, u32[]{:S(2)}, u32[]{:S(2)}) async-start(bf16[512,4,1024]{2,0,1:T(8,128)(2,1)} %bitcast.159), calls=%async_computation.3 | async-start | bytes 8388608 | tf_op jit(solution)/shard_map/all_to_all | solution.py:53
  41.5 173.5 %all-gather.3.cloned.1.call-start = ((), (), s32[]{:S(2)}) async-start(), calls=%async_computation.5 | async-start | bytes 4259840 | tf_op jit(solution)/shard_map/all_gather | solution.py:31
  86.3 131.1 %all-to-all-start.2 = ((bf16[64,1,128,256]{3,2,1,0:T(8,128)(2,1)}), bf16[64,1,128,256]{3,2,1,0:T(8,128)(2,1)}, u32[]{:S(2)}, u32[]{:S(2)}) async-start(bf16[64,1,128,256]{3,2,1,0:T(8,128)(2,1)} %fusion.16), calls=%async_computation.2 | async-start | bytes 8388608 | tf_op jit(solution)/shard_map/all_to_all | solution.py:92
  105.5 9.0 %collective-permute-start = (bf16[128,256]{1,0:T(8,128)(2,1)S(1)}, bf16[128,256]{1,0:T(8,128)(2,1)S(1)}, u32[]{:S(2)}, u32[]{:S(2)}) collective-permute-start(bf16[128,256]{1,0:T(8,128)(2,1)S(1)} %get-tuple-element.79), channel_id=1, source_target_pairs={{0,4},{4,8},{8,12},{12,16},{16,20},{20,24},{24,28},{28,32},{32,36}... | collective-permute-start | bytes 196616 | tf_op jit(solution)/shard_map/ppermute | solution.py:21
  109.0 8.1 %collective-permute-start.1 = (bf16[128,256]{1,0:T(8,128)(2,1)S(1)}, bf16[128,256]{1,0:T(8,128)(2,1)S(1)}, u32[]{:S(2)}, u32[]{:S(2)}) collective-permute-start(bf16[128,256]{1,0:T(8,128)(2,1)S(1)} %get-tuple-element.78), channel_id=1, source_target_pairs={{4,0},{8,4},{12,8},{16,12},{20,16},{24,20},{28,24},{32,28},{36,32}... | collective-permute-start | bytes 196616 | tf_op jit(solution)/shard_map/ppermute | solution.py:23
  359.9 6.4 %copy-start.1 = (bf16[512,512]{1,0:T(8,128)(2,1)S(1)}, bf16[512,512]{1,0:T(8,128)(2,1)}, u32[]{:S(2)}) copy-start(bf16[512,512]{1,0:T(8,128)(2,1)} %param.8) | copy-start | bytes 1572868
Sparse Core Ops, SparseCore 0:
  32.0 88.4 all-gather.4
  123.2 91.6 all-gather.2
where the time goes:
time: 375 us; the launch traced here: 373 us
  waiting for transfers between devices  137 us (37%)
  local copies, waits for them, and re-layouts  72.6 us (19%)
  blocking collectives  54.3 us (14%)
  starting transfers between devices  36.7 us (10%)
  matrix products  31.9 us (9%)
  other arithmetic  22.1 us (6%)
  between operations  18.8 us (5%)
    all_gather x2, waiting for transfers between devices, picked(): lax.all_gather(shard, axis)  88.3 us
    all_to_all x1, blocking collectives, on_device(): lax.all_to_all(output_rows, 'head', split_axis=0, concat_axis=1, tiled=True)  54.3 us
    all_to_all x1, waiting for transfers between devices, on_device(): lax.all_to_all(query_rows, 'head', split_axis=1, concat_axis=0, tiled=True)  35.6 us
    all_to_all x3, local copies, waits for them, and re-layouts, on_device(): lax.all_to_all(output_rows, 'head', split_axis=0, concat_axis=1, tiled=True)  20 us
    dot_general x4, matrix products, attend_group(): jnp.einsum('pgts,psd->ptgd', rounded, values, preferred_element_type=jnp....  19.8 us
    all_to_all x1, starting transfers between devices, on_device(): lax.all_to_all(outgoing, 'seq', split_axis=0, concat_axis=0, tiled=True)  17.9 us
    reduce_sum x4, other arithmetic, attend_group(): row_total = jnp.sum(weights, axis=-1)  15 us
    dot_general x4, matrix products, attend_group(): jnp.einsum('ptgd,psd->pgts', query_group, key_part, preferred_element_typ...  12.1 us
  transfers between devices with their start and end apart: 8, of which 6 were waited for; matrix products, arithmetic and copies ran while one was open for 8% of the time, Pallas kernels for 0%

commit v1 on v0

--- a/solution.py
+++ b/solution.py
@@ -50,7 +50,12 @@
 
 def on_device(query_rows, key_rows, value_rows, random_table, global_blocks):
     queries, key_part, values = (
-        lax.all_to_all(query_rows, "head", split_axis=1, concat_axis=0, tiled=True),
+        jnp.concatenate(
+            lax.all_to_all(
+                jnp.stack(jnp.split(query_rows, lax.axis_size("head"), 1), axis=0), "head", 0, 0
+            ),
+            0,
+        ),
         lax.all_to_all(key_rows, "head", split_axis=1, concat_axis=0, tiled=True),
         lax.all_to_all(value_rows, "head", split_axis=1, concat_axis=0, tiled=True),
     )

time: 375 us -> 375 us (level)
    all_to_all x1 -> x0, local copies, waits for them, and re-layouts: 4.72 us -> none  [on_device(): lax.all_to_all(query_rows, 'head', split_axis=1, concat_axis=0, tiled=True)]
where the time goes in v1:
time: 375 us; the launch traced here: 373 us
  waiting for transfers between devices  137 us (37%)
  local copies, waits for them, and re-layouts  70.5 us (19%)
  blocking collectives  54.3 us (14%)
  starting transfers between devices  36.6 us (10%)
  matrix products  31.9 us (9%)
  other arithmetic  24.3 us (6%)
  between operations  18.6 us (5%)
    all_gather x2, waiting for transfers between devices, picked(): lax.all_gather(shard, axis)  88.3 us
    all_to_all x1, blocking collectives, on_device(): lax.all_to_all(output_rows, 'head', split_axis=0, concat_axis=1, tiled=True)  54.3 us
    all_to_all x1, waiting for transfers between devices, on_device(): lax.all_to_all(jnp.stack(jnp.split(query_rows, lax.axis_size('head'), 1),...  35.6 us
    all_to_all x3, local copies, waits for them, and re-layouts, on_device(): lax.all_to_all(output_rows, 'head', split_axis=0, concat_axis=1, tiled=True)  20 us
    dot_general x4, matrix products, attend_group(): jnp.einsum('pgts,psd->ptgd', rounded, values, preferred_element_type=jnp....  19.8 us
    all_to_all x1, starting transfers between devices, on_device(): lax.all_to_all(outgoing, 'seq', split_axis=0, concat_axis=0, tiled=True)  17.9 us
    reduce_sum x4, other arithmetic, attend_group(): row_total = jnp.sum(weights, axis=-1)  15 us
    dot_general x4, matrix products, attend_group(): jnp.einsum('ptgd,psd->pgts', query_group, key_part, preferred_element_typ...  12.1 us
  transfers between devices with their start and end apart: 8, of which 6 were waited for; matrix products, arithmetic and copies ran while one was open for 8% of the time, Pallas kernels for 0%

profile of v1, /device:TPU:1, one launch (start us, length us, event | category | flops | bytes accessed | tf_op | source)
XLA Modules:
  0.0 373.3 jit_solution(11673147134487753812)
XLA Ops:
  8.5 4.8 %all-to-all-start = ((bf16[512,4,128]{2,0,1:T(8,128)(2,1)}), bf16[512,4,128]{2,0,1:T(8,128)(2,1)S(1)}, u32[]{:S(2)}, u32[]{:S(2)}) async-start(bf16[512,4,128]{2,0,1:T(8,128)(2,1)} %copy_bitcast_fusion.3), calls=%async_computation | async-start | bytes 1048576 | tf_op jit(solution)/shard_map/all_to_all | solution.py:59
  15.2 5.5 %all-to-all-done = bf16[512,4,128]{2,0,1:T(8,128)(2,1)S(1)} async-done(((bf16[512,4,128]{2,0,1:T(8,128)(2,1)}), bf16[512,4,128]{2,0,1:T(8,128)(2,1)S(1)}, u32[]{:S(2)}, u32[]{:S(2)}) %all-to-all-start) | async-done | bytes 524320 | tf_op jit(solution)/shard_map/all_to_all | solution.py:59
  20.8 3.5 all-to-all-start.1
  31.8 2.6 slice_bitcast_fusion.7
  36.7 4.9 %all-to-all-start.3 = ((bf16[4,512,1024]{2,1,0:T(8,128)(2,1)}), bf16[4,512,1024]{2,1,0:T(8,128)(2,1)}, u32[]{:S(2)}, u32[]{:S(2)}) async-start(bf16[4,512,1024]{2,1,0:T(8,128)(2,1)} %pad_maximum_fusion), calls=%async_computation.3 | async-start | bytes 8388608 | tf_op jit(solution)/shard_map/all_to_all | solution.py:54
  44.0 2.8 gather_fusion
  46.8 4.0 %fusion.16 = bf16[64,1,128,256]{3,2,1,0:T(8,128)(2,1)} fusion(bf16[64,128,256]{2,1,0:T(8,128)(2,1)} %gather_fusion, pred[64]{0:T(512)(128)(4,1)S(1)} %compare_and_fusion, pred[64]{0:T(512)(128)(4,1)S(1)} %get-tuple-element.70), kind=kLoop, calls=%fused_computation.27 | loop fusion | flops 4194304 | bytes 8388736 | tf_op jit(solution)/shard_map/jit(_where)/select_n | solution.py:96
  50.8 35.6 %all-to-all-done.3 = bf16[4,512,1024]{2,1,0:T(8,128)(2,1)} async-done(((bf16[4,512,1024]{2,1,0:T(8,128)(2,1)}), bf16[4,512,1024]{2,1,0:T(8,128)(2,1)}, u32[]{:S(2)}, u32[]{:S(2)}) %all-to-all-start.3) | async-done | bytes 4194336 | tf_op jit(solution)/shard_map/all_to_all | solution.py:54
  86.4 17.9 %all-to-all-start.2 = ((bf16[64,1,128,256]{3,2,1,0:T(8,128)(2,1)}), bf16[64,1,128,256]{3,2,1,0:T(8,128)(2,1)}, u32[]{:S(2)}, u32[]{:S(2)}) async-start(bf16[64,1,128,256]{3,2,1,0:T(8,128)(2,1)} %fusion.16), calls=%async_computation.2 | async-start | bytes 8388608 | tf_op jit(solution)/shard_map/all_to_all | solution.py:97
  105.6 3.5 collective-permute-start
  114.6 2.8 collective-permute-done.1
  120.7 5.2 %copy.76 = bf16[256,8,8,128]{3,2,1,0:T(8,128)(2,1)} copy(bf16[256,8,8,128]{3,1,2,0:T(8,128)(2,1)} %bitcast.54) | data formatting | bytes 8388608
  126.8 88.3 %all-gather.3.cloned.1.call-done = bf16[64,128,256]{2,1,0:T(8,128)(2,1)} async-done(((bf16[1,128,256]{2,1,0:T(8,128)(2,1)}), bf16[64,128,256]{2,1,0:T(8,128)(2,1)}) %all-gather.3.cloned.1.call-update) | async-done | bytes 4194320 | tf_op jit(solution)/shard_map/all_gather | solution.py:31
  217.5 4.7 %gather_fusion.2 = bf16[48,128,256]{2,1,0:T(8,128)(2,1)} fusion(bf16[64,1,128,256]{3,2,1,0:T(8,128)(2,1)} %all-to-all-done.2, s32[48]{0:T(128)S(1)} %fusion.35), kind=kCustom, calls=%fused_computation.2 | custom fusion | bytes 6291840 | tf_op jit(solution)/shard_map/gather | solution.py:105
  222.1 3.8 %constant_dynamic-update-slice_fusion.1 = bf16[4,4,1024,256]{3,2,1,0:T(8,128)(2,1)} fusion(bf16[4,4,1024,256]{3,2,1,0:T(8,128)(2,1)} %broadcast_dynamic-update-slice_fusion, bf16[4,4,384,256]{3,2,1,0:T(8,128)(2,1)} %bitcast.164), kind=kLoop, calls=%fused_computation.70 | loop fusion | bytes 6291456 | tf_op jit(solution)/shard_map/concatenate | solution.py:112
  226.0 66.2 %while.10 = (s32[]{:T(128)}, bf16[4,4,128,8,128]{4,3,2,1,0:T(8,128)(2,1)}, bf16[4,4,1024,256]{3,2,1,0:T(8,128)(2,1)}, pred[4,4,1024]{2,1,0:T(4,128)(4,1)S(1)}, bf16[4,4,128,8,128]{4,3,2,1,0:T(8,128)(2,1)}, /*index=5*/s32[]{:T(128)}) while((s32[]{:T(128)}, bf16[4,4,128,8,128]{4,3,2,1,0:T(8,128)(2,1)}, bf16[4,4,1024,256]{3,2,1,0:T(8,128)(2,1)}, ...), condition=%wide.region_9.10_spmd, body=%wide.region_6.9_spmd.sunk | while | flops 2194661376 | bytes 65114704 | solution.py:134
  229.0 3.0 bitcast_reduce_fusion.2
  232.1 3.7 %fusion.48 = f32[4,8,128]{2,1,0:T(8,128)S(1)} fusion(f32[4,1024,128,8]{2,1,3,0:T(8,128)S(1)} %get-tuple-element.121, f32[4,8,128]{2,1,0:T(8,128)S(1)} %get-tuple-element.122, pred[4,1024]{1,0:T(4,128)(4,1)S(1)} %dynamic-slice_bitcast_fusion.4), kind=kLoop, calls=%fused_computation.7.clone.1 | loop fusion | flops 16773120 | bytes 16814080 | tf_op jit(solution)/shard_map/while/body/eval_jaxpr/reduce_sum | solution.py:44
  235.8 5.0 %fusion.49 = bf16[1,4,128,8,128]{2,4,3,1,0:T(8,128)(2,1)S(1)} fusion(f32[4,1024,128,8]{2,1,3,0:T(8,128)S(1)} %get-tuple-element.121, f32[4,8,128]{2,1,0:T(8,128)S(1)} %get-tuple-element.122, pred[4,1024]{1,0:T(4,128)(4,1)S(1)} %dynamic-slice_bitcast_fusion.4, bf16[4,1024,256]{2,1,0:T(8,128)(2,1)S(1)} %dynamic-slice_bitcast_fusion.5, ...), kind=kOutput, calls=%fused_computation.14.clone.1 | convolution fusion | flops 1091567616 | bytes 18911232 | tf_op jit(solution)/shard_map/while/body/eval_jaxpr/pgts,psd->ptgd/dot_general | solution.py:46
  245.6 3.0 bitcast_reduce_fusion.2
  248.6 3.7 %fusion.48 = f32[4,8,128]{2,1,0:T(8,128)S(1)} fusion(f32[4,1024,128,8]{2,1,3,0:T(8,128)S(1)} %get-tuple-element.121, f32[4,8,128]{2,1,0:T(8,128)S(1)} %get-tuple-element.122, pred[4,1024]{1,0:T(4,128)(4,1)S(1)} %dynamic-slice_bitcast_fusion.4), kind=kLoop, calls=%fused_computation.7.clone.1 | loop fusion | flops 16773120 | bytes 16814080 | tf_op jit(solution)/shard_map/while/body/eval_jaxpr/reduce_sum | solution.py:44
  252.4 5.0 %fusion.49 = bf16[1,4,128,8,128]{2,4,3,1,0:T(8,128)(2,1)S(1)} fusion(f32[4,1024,128,8]{2,1,3,0:T(8,128)S(1)} %get-tuple-element.121, f32[4,8,128]{2,1,0:T(8,128)S(1)} %get-tuple-element.122, pred[4,1024]{1,0:T(4,128)(4,1)S(1)} %dynamic-slice_bitcast_fusion.4, bf16[4,1024,256]{2,1,0:T(8,128)(2,1)S(1)} %dynamic-slice_bitcast_fusion.5, ...), kind=kOutput, calls=%fused_computation.14.clone.1 | convolution fusion | flops 1091567616 | bytes 18911232 | tf_op jit(solution)/shard_map/while/body/eval_jaxpr/pgts,psd->ptgd/dot_general | solution.py:46
  262.1 3.0 bitcast_reduce_fusion.2
  265.2 3.7 %fusion.48 = f32[4,8,128]{2,1,0:T(8,128)S(1)} fusion(f32[4,1024,128,8]{2,1,3,0:T(8,128)S(1)} %get-tuple-element.121, f32[4,8,128]{2,1,0:T(8,128)S(1)} %get-tuple-element.122, pred[4,1024]{1,0:T(4,128)(4,1)S(1)} %dynamic-slice_bitcast_fusion.4), kind=kLoop, calls=%fused_computation.7.clone.1 | loop fusion | flops 16773120 | bytes 16814080 | tf_op jit(solution)/shard_map/while/body/eval_jaxpr/reduce_sum | solution.py:44
  268.9 5.0 %fusion.49 = bf16[1,4,128,8,128]{2,4,3,1,0:T(8,128)(2,1)S(1)} fusion(f32[4,1024,128,8]{2,1,3,0:T(8,128)S(1)} %get-tuple-element.121, f32[4,8,128]{2,1,0:T(8,128)S(1)} %get-tuple-element.122, pred[4,1024]{1,0:T(4,128)(4,1)S(1)} %dynamic-slice_bitcast_fusion.4, bf16[4,1024,256]{2,1,0:T(8,128)(2,1)S(1)} %dynamic-slice_bitcast_fusion.5, ...), kind=kOutput, calls=%fused_computation.14.clone.1 | convolution fusion | flops 1091567616 | bytes 18911232 | tf_op jit(solution)/shard_map/while/body/eval_jaxpr/pgts,psd->ptgd/dot_general | solution.py:46
  278.7 3.0 bitcast_reduce_fusion.2
  281.7 3.7 %fusion.48 = f32[4,8,128]{2,1,0:T(8,128)S(1)} fusion(f32[4,1024,128,8]{2,1,3,0:T(8,128)S(1)} %get-tuple-element.121, f32[4,8,128]{2,1,0:T(8,128)S(1)} %get-tuple-element.122, pred[4,1024]{1,0:T(4,128)(4,1)S(1)} %dynamic-slice_bitcast_fusion.4), kind=kLoop, calls=%fused_computation.7.clone.1 | loop fusion | flops 16773120 | bytes 16814080 | tf_op jit(solution)/shard_map/while/body/eval_jaxpr/reduce_sum | solution.py:44
  285.5 5.0 %fusion.49 = bf16[1,4,128,8,128]{2,4,3,1,0:T(8,128)(2,1)S(1)} fusion(f32[4,1024,128,8]{2,1,3,0:T(8,128)S(1)} %get-tuple-element.121, f32[4,8,128]{2,1,0:T(8,128)S(1)} %get-tuple-element.122, pred[4,1024]{1,0:T(4,128)(4,1)S(1)} %dynamic-slice_bitcast_fusion.4, bf16[4,1024,256]{2,1,0:T(8,128)(2,1)S(1)} %dynamic-slice_bitcast_fusion.5, ...), kind=kOutput, calls=%fused_computation.14.clone.1 | convolution fusion | flops 1091567616 | bytes 18911232 | tf_op jit(solution)/shard_map/while/body/eval_jaxpr/pgts,psd->ptgd/dot_general | solution.py:46
  292.2 7.3 %all_to_all.58 = bf16[4,512,1024]{2,1,0:T(8,128)(2,1)} reshape(bf16[4,4,128,8,128]{4,3,2,1,0:T(8,128)(2,1)} %get-tuple-element.32) | data formatting | bytes 8388608 | tf_op jit(solution)/shard_map/all_to_all | solution.py:136
  299.5 54.3 %all_to_all.67 = bf16[4,512,1024]{2,1,0:T(8,128)(2,1)} all-to-all(bf16[4,512,1024]{2,1,0:T(8,128)(2,1)} %all_to_all.58), channel_id=1, replica_groups=mesh['seq'=64,'head'=4] {'head'}, dimensions={0} | all-to-all | bytes 8388608 | tf_op jit(solution)/shard_map/all_to_all | solution.py:136
  353.8 6.3 %copy.64 = bf16[512,4,1024]{0,2,1:T(8,128)(2,1)} copy(bf16[512,4,1024]{2,0,1:T(8,128)(2,1)} %bitcast.162) | data formatting | bytes 8388608 | tf_op jit(solution)/shard_map/all_to_all | solution.py:136
  360.1 6.4 %copy.65 = bf16[512,4096]{1,0:T(8,128)(2,1)} copy(bf16[512,4096]{0,1:T(8,128)(2,1)} %bitcast.163) | data formatting | bytes 8388608 | tf_op jit(solution)/shard_map/all_to_all | solution.py:136
  (82 shorter events, 43.3 us)
Async XLA Ops:
  6.5 1.0 copy-start
  6.5 17.8 %copy-start.2 = (s32[2]{0:T(128)S(1)}, s32[2]{0:T(128)}, u32[]{:S(2)}) copy-start(s32[2]{0:T(128)} %param.11) | copy-start | bytes 28
  8.5 12.3 %all-to-all-start = ((bf16[512,4,128]{2,0,1:T(8,128)(2,1)}), bf16[512,4,128]{2,0,1:T(8,128)(2,1)S(1)}, u32[]{:S(2)}, u32[]{:S(2)}) async-start(bf16[512,4,128]{2,0,1:T(8,128)(2,1)} %copy_bitcast_fusion.3), calls=%async_computation | async-start | bytes 1048576 | tf_op jit(solution)/shard_map/all_to_all | solution.py:59
  20.8 10.4 %all-to-all-start.1 = ((bf16[512,4,128]{2,0,1:T(8,128)(2,1)}), bf16[512,4,128]{2,0,1:T(8,128)(2,1)S(1)}, u32[]{:S(2)}, u32[]{:S(2)}) async-start(bf16[512,4,128]{2,0,1:T(8,128)(2,1)} %copy_bitcast_fusion.2), calls=%async_computation.1 | async-start | bytes 1048576 | tf_op jit(solution)/shard_map/all_to_all | solution.py:60
  24.2 101.7 %all-gather.5.cloned.1.call-start = ((), (), s32[]{:S(2)}) async-start(), calls=%async_computation.6 | async-start | bytes 4259840 | tf_op jit(solution)/shard_map/all_gather | solution.py:31
  36.7 49.7 %all-to-all-start.3 = ((bf16[4,512,1024]{2,1,0:T(8,128)(2,1)}), bf16[4,512,1024]{2,1,0:T(8,128)(2,1)}, u32[]{:S(2)}, u32[]{:S(2)}) async-start(bf16[4,512,1024]{2,1,0:T(8,128)(2,1)} %pad_maximum_fusion), calls=%async_computation.3 | async-start | bytes 8388608 | tf_op jit(solution)/shard_map/all_to_all | solution.py:54
  41.6 173.5 %all-gather.3.cloned.1.call-start = ((), (), s32[]{:S(2)}) async-start(), calls=%async_computation.5 | async-start | bytes 4259840 | tf_op jit(solution)/shard_map/all_gather | solution.py:31
  86.4 131.1 %all-to-all-start.2 = ((bf16[64,1,128,256]{3,2,1,0:T(8,128)(2,1)}), bf16[64,1,128,256]{3,2,1,0:T(8,128)(2,1)}, u32[]{:S(2)}, u32[]{:S(2)}) async-start(bf16[64,1,128,256]{3,2,1,0:T(8,128)(2,1)} %fusion.16), calls=%async_computation.2 | async-start | bytes 8388608 | tf_op jit(solution)/shard_map/all_to_all | solution.py:97
  105.6 9.0 %collective-permute-start = (bf16[128,256]{1,0:T(8,128)(2,1)S(1)}, bf16[128,256]{1,0:T(8,128)(2,1)S(1)}, u32[]{:S(2)}, u32[]{:S(2)}) collective-permute-start(bf16[128,256]{1,0:T(8,128)(2,1)S(1)} %get-tuple-element.83), channel_id=1, source_target_pairs={{0,4},{4,8},{8,12},{12,16},{16,20},{20,24},{24,28},{28,32},{32,36}... | collective-permute-start | bytes 196616 | tf_op jit(solution)/shard_map/ppermute | solution.py:21
  109.2 8.2 %collective-permute-start.1 = (bf16[128,256]{1,0:T(8,128)(2,1)S(1)}, bf16[128,256]{1,0:T(8,128)(2,1)S(1)}, u32[]{:S(2)}, u32[]{:S(2)}) collective-permute-start(bf16[128,256]{1,0:T(8,128)(2,1)S(1)} %get-tuple-element.82), channel_id=1, source_target_pairs={{4,0},{8,4},{12,8},{16,12},{20,16},{24,20},{28,24},{32,28},{36,32}... | collective-permute-start | bytes 196616 | tf_op jit(solution)/shard_map/ppermute | solution.py:23
  360.1 6.4 %copy-start.1 = (bf16[512,512]{1,0:T(8,128)(2,1)S(1)}, bf16[512,512]{1,0:T(8,128)(2,1)}, u32[]{:S(2)}) copy-start(bf16[512,512]{1,0:T(8,128)(2,1)} %param.8) | copy-start | bytes 1572868
Sparse Core Ops, SparseCore 0:
  31.9 88.4 all-gather.4
  123.2 91.8 all-gather.2
